TPU v7x, 32 devices: a whole 2x2x4 slice. The times are simulated.
32 devices in a mesh: seq: 4 (over z), fsdp: 8 (over y, x, core).
Axes of the slice: x: 2, y: 2, z: 4, core: 2. Of those that a mesh axis runs over, the one named last changes fastest.
Arguments:
- tokens: float32 [16, 1024, 1536], P('fsdp', 'seq'), may hold values from -6 to 6
- cotangent: float32 [16, 1024, 1536], P('fsdp', 'seq'), may hold values from -6 to 6
- attention_gain: bfloat16 [1536], P('fsdp'), may hold values from 0.5 to 1.5
- feedforward_gain: bfloat16 [1536], P('fsdp'), may hold values from 0.5 to 1.5
- query_weight: bfloat16 [1536, 1536], P('fsdp'), may hold values from -1 to 1
- key_matrix: bfloat16 [1536, 768], P('fsdp'), may hold values from -16 to 16
- value_matrix: bfloat16 [1536, 768], P('fsdp'), may hold values from -0.15625 to 0.15625
- out_weight: bfloat16 [1536, 1536], P('fsdp'), may hold values from -1.25 to 1.25
- gate_weight: bfloat16 [1536, 4096], P('fsdp'), may hold values from -0.15625 to 0.15625
- up_weight: bfloat16 [1536, 4096], P('fsdp'), may hold values from -0.15625 to 0.15625
- down_weight: bfloat16 [4096, 1536], P('fsdp'), may hold values from -0.09375 to 0.09375
Outputs:
- block_out: float32 [16, 1024, 1536], P('fsdp', 'seq')
- grad_tokens: float32 [16, 1024, 1536], P('fsdp', 'seq')
- grad_attention_gain: float32 [1536], P('fsdp')
- grad_feedforward_gain: float32 [1536], P('fsdp')
- grad_query: float32 [1536, 1536], P('fsdp')
- grad_key: float32 [1536, 768], P('fsdp')
- grad_value: float32 [1536, 768], P('fsdp')
- grad_out: float32 [1536, 1536], P('fsdp')
- grad_gate: float32 [1536, 4096], P('fsdp')
- grad_up: float32 [1536, 4096], P('fsdp')
- grad_down: float32 [4096, 1536], P('fsdp')
All inputs are finite; a program needn't handle non-finite values.
Results may differ from a plain program's by a relative error of at most 0.024.
The roundings to bfloat16 on the way count: a program that leaves them out, or rounds other values in their place, can miss the bound.
Values may be sent and summed in bfloat16 or wider, within the bound.
A program may use at most 320 MiB of HBM per device.

v0:
```python
from functools import partial
import math
import jax
import jax.numpy as jnp
from jax import lax
from jax.sharding import PartitionSpec as P

QUERY_HEADS = 16
KEY_VALUE_HEADS = 8
HEAD_DIM = 96
norm_eps = 1e-05
rope_base = 100000.0
masked_score = -1e30


def rope_tables(positions, head_size):
    half = head_size // 2
    freqs = rope_base ** (-(2.0 * jnp.arange(half, dtype=jnp.float32)) / head_size)
    angles = positions.astype(jnp.float32)[:, None] * freqs[None, :]
    return (jnp.cos(angles), jnp.sin(angles))


def rotate_halves(values, cosine, sine):
    half = values.shape[-1] // 2
    first = values[..., :half]
    second = values[..., half:]
    return jnp.concatenate(
        [first * cosine - second * sine, second * cosine + first * sine], axis=-1
    )


def reverse_rotation(grads, cosine, sine):
    half = grads.shape[-1] // 2
    first = grads[..., :half]
    second = grads[..., half:]
    return jnp.concatenate(
        [first * cosine + second * sine, second * cosine - first * sine], axis=-1
    )


def masked_scores(query_rows, key_rows, scale):
    sequence_length = query_rows.shape[0]
    scores = (
        jnp.einsum("qhgd,khd->hgqk", query_rows, key_rows, preferred_element_type=jnp.float32)
        * scale
    )
    causal = jnp.arange(sequence_length)[:, None] >= jnp.arange(sequence_length)[None, :]
    return jnp.where(causal, scores, masked_score)


def attend_items(packed_arrays, group_size, head_size):
    count, sequence_length, features = packed_arrays.shape
    kv_local = features // ((group_size + 2) * head_size)
    scale = 1.0 / math.sqrt(head_size)

    def single(item):
        split = item.reshape(sequence_length, kv_local, group_size + 2, head_size)
        query_rows = split[:, :, :group_size, :]
        key_rows = split[:, :, group_size, :]
        value_matrix_rows = split[:, :, group_size + 1, :]
        scores = masked_scores(query_rows, key_rows, scale)
        top_score = jnp.max(scores, axis=-1, keepdims=True)
        log_total = top_score + jnp.log(
            jnp.sum(jnp.exp(scores - top_score), axis=-1, keepdims=True)
        )
        probs = jnp.exp(scores - log_total).astype(jnp.bfloat16)
        attended = jnp.einsum(
            "hgqk,khd->qhgd", probs, value_matrix_rows, preferred_element_type=jnp.float32
        )
        return (
            attended.astype(jnp.bfloat16).reshape(
                sequence_length, kv_local * group_size * head_size
            ),
            log_total[..., 0],
        )

    attended_all, log_totals = lax.map(single, packed_arrays)
    return (attended_all, log_totals, packed_arrays)


def attend_back_item(inputs, group_size, head_size, cosine, sine):
    packed_item, attended_item, log_total, grad_item = inputs
    sequence_length = packed_item.shape[0]
    kv_local = packed_item.shape[1] // ((group_size + 2) * head_size)
    scale = 1.0 / math.sqrt(head_size)
    split = packed_item.reshape(sequence_length, kv_local, group_size + 2, head_size)
    query_rows = split[:, :, :group_size, :]
    key_rows = split[:, :, group_size, :]
    value_matrix_rows = split[:, :, group_size + 1, :]
    out_heads = attended_item.reshape(sequence_length, kv_local, group_size, head_size)
    grad_heads = grad_item.reshape(sequence_length, kv_local, group_size, head_size)
    scores = masked_scores(query_rows, key_rows, scale)
    probs = jnp.exp(scores - log_total[..., None])
    delta = jnp.einsum("qhgd,qhgd->hgq", grad_heads, out_heads, preferred_element_type=jnp.float32)
    value_gradients = jnp.einsum(
        "hgqk,qhgd->khd", probs.astype(jnp.bfloat16), grad_heads, preferred_element_type=jnp.float32
    )
    grad_probs = jnp.einsum(
        "qhgd,khd->hgqk", grad_heads, value_matrix_rows, preferred_element_type=jnp.float32
    )
    grad_scores = (probs * (grad_probs - delta[..., None]) * scale).astype(jnp.bfloat16)
    grad_queries = jnp.einsum(
        "hgqk,khd->qhgd", grad_scores, key_rows, preferred_element_type=jnp.float32
    )
    key_gradients = jnp.einsum(
        "hgqk,qhgd->khd", grad_scores, query_rows, preferred_element_type=jnp.float32
    )
    grad_queries = reverse_rotation(grad_queries, cosine[:, None, None, :], sine[:, None, None, :])
    key_gradients = reverse_rotation(key_gradients, cosine[:, None, :], sine[:, None, :])
    stacked = jnp.concatenate(
        [
            grad_queries.astype(jnp.bfloat16),
            key_gradients.astype(jnp.bfloat16)[:, :, None, :],
            value_gradients.astype(jnp.bfloat16)[:, :, None, :],
        ],
        axis=2,
    )
    return stacked.reshape(sequence_length, kv_local * (group_size + 2) * head_size)


def norm_back(grad_normed, normed, inverse, gain):
    scaled = grad_normed * gain
    return inverse * (scaled - normed * jnp.mean(scaled * normed, axis=-1, keepdims=True))


def body(
    tokens,
    cotangent,
    attention_gain,
    feedforward_gain,
    query_weight,
    key_matrix,
    value_matrix,
    out_weight,
    gate_weight,
    up_weight,
    down_weight,
):
    sequence_count, span_length, width = tokens.shape
    row_count = sequence_count * span_length
    group_size = QUERY_HEADS // KEY_VALUE_HEADS
    gain_low_one, gain_low_two, whole_query, whole_key, whole_value, whole_out = (
        lax.all_gather(attention_gain, "fsdp", axis=0, tiled=True),
        lax.all_gather(feedforward_gain, "fsdp", axis=0, tiled=True),
        lax.all_gather(query_weight, "fsdp", axis=0, tiled=True),
        lax.all_gather(key_matrix, "fsdp", axis=0, tiled=True),
        lax.all_gather(value_matrix, "fsdp", axis=0, tiled=True),
        lax.all_gather(out_weight, "fsdp", axis=0, tiled=True),
    )
    gain_one = gain_low_one.astype(jnp.float32)
    gain_two = gain_low_two.astype(jnp.float32)
    positions = lax.axis_index("seq") * span_length + jnp.arange(span_length, dtype=jnp.int32)
    cosine, sine = rope_tables(positions, HEAD_DIM)
    cosine_rows = jnp.tile(cosine, (sequence_count, 1))[:, None, :]
    sine_rows = jnp.tile(sine, (sequence_count, 1))[:, None, :]
    flat = tokens.reshape(row_count, width)
    inv_one = lax.rsqrt(jnp.mean(flat * flat, axis=-1, keepdims=True) + norm_eps)
    normed_one = flat * inv_one
    first_inputs = (normed_one * gain_one).astype(jnp.bfloat16)
    query_projected = jnp.dot(
        first_inputs, whole_query, preferred_element_type=jnp.float32
    ).reshape(row_count, QUERY_HEADS, HEAD_DIM)
    key_projected = jnp.dot(first_inputs, whole_key, preferred_element_type=jnp.float32).reshape(
        row_count, KEY_VALUE_HEADS, HEAD_DIM
    )
    value_matrix_rows = jnp.dot(
        first_inputs, whole_value, preferred_element_type=jnp.float32
    ).astype(jnp.bfloat16)
    query_rotated = (
        rotate_halves(query_projected, cosine_rows, sine_rows)
        .astype(jnp.bfloat16)
        .reshape(row_count, KEY_VALUE_HEADS, group_size, HEAD_DIM)
    )
    key_rotated = (
        rotate_halves(key_projected, cosine_rows, sine_rows)
        .astype(jnp.bfloat16)
        .reshape(row_count, KEY_VALUE_HEADS, 1, HEAD_DIM)
    )
    packed_arrays = jnp.concatenate(
        [
            query_rotated,
            key_rotated,
            value_matrix_rows.reshape(row_count, KEY_VALUE_HEADS, 1, HEAD_DIM),
        ],
        axis=2,
    )
    packed_arrays = packed_arrays.reshape(
        sequence_count, span_length, KEY_VALUE_HEADS * (group_size + 2) * HEAD_DIM
    )
    attend_fn = partial(attend_items, group_size=group_size, head_size=HEAD_DIM)
    heads_attended, log_totals, head_inputs = attend_fn(
        lax.all_to_all(packed_arrays, "seq", split_axis=2, concat_axis=1, tiled=True)
    )
    attended_flat = lax.all_to_all(
        heads_attended, "seq", split_axis=1, concat_axis=2, tiled=True
    ).reshape(row_count, QUERY_HEADS * HEAD_DIM)
    hidden_one = flat + jnp.dot(attended_flat, whole_out, preferred_element_type=jnp.float32)
    inv_two = lax.rsqrt(jnp.mean(hidden_one * hidden_one, axis=-1, keepdims=True) + norm_eps)
    normed_two = hidden_one * inv_two
    inputs_two = (normed_two * gain_two).astype(jnp.bfloat16)
    pieces = (
        lax.all_gather(gate_weight, "fsdp", axis=0, tiled=True),
        lax.all_gather(up_weight, "fsdp", axis=0, tiled=True),
    )
    columns = inputs_two
    gate_pre = jnp.dot(columns, pieces[0], preferred_element_type=jnp.float32)
    up_pre = jnp.dot(columns, pieces[1], preferred_element_type=jnp.float32)
    sigmoid_gate = jax.nn.sigmoid(gate_pre)
    hidden_act = (gate_pre * sigmoid_gate * up_pre).astype(jnp.bfloat16)
    columns = hidden_act
    ffn_result = jnp.dot(
        columns,
        lax.all_gather(down_weight, "fsdp", axis=0, tiled=True),
        preferred_element_type=jnp.float32,
    )
    block_out = hidden_one + ffn_result
    grad_flat = cotangent.reshape(row_count, width)
    grad_low = grad_flat.astype(jnp.bfloat16)
    grad_down = jnp.dot(hidden_act.T, grad_low, preferred_element_type=jnp.float32)
    grad_hidden = jnp.dot(
        grad_low,
        lax.all_gather(down_weight, "fsdp", axis=0, tiled=True).T,
        preferred_element_type=jnp.float32,
    )
    grad_gate_pre = (
        grad_hidden * up_pre * sigmoid_gate * (1.0 + gate_pre * (1.0 - sigmoid_gate))
    ).astype(jnp.bfloat16)
    grad_up_pre = (grad_hidden * gate_pre * sigmoid_gate).astype(jnp.bfloat16)
    grad_gate = jnp.dot(inputs_two.T, grad_gate_pre, preferred_element_type=jnp.float32)
    grad_up = jnp.dot(inputs_two.T, grad_up_pre, preferred_element_type=jnp.float32)
    pieces = (
        lax.all_gather(gate_weight, "fsdp", axis=0, tiled=True),
        lax.all_gather(up_weight, "fsdp", axis=0, tiled=True),
    )
    block = jnp.dot(grad_gate_pre, pieces[0].T, preferred_element_type=jnp.float32) + jnp.dot(
        grad_up_pre, pieces[1].T, preferred_element_type=jnp.float32
    )
    gain_grad_two = jnp.sum(block * normed_two, axis=0)
    grad_hidden_one = grad_flat + norm_back(block, normed_two, inv_two, gain_two)
    ffn_shards = (
        lax.psum_scatter(
            gain_grad_two.astype(jnp.bfloat16), "fsdp", scatter_dimension=0, tiled=True
        ).astype(jnp.float32),
        lax.psum_scatter(
            grad_gate.astype(jnp.bfloat16), "fsdp", scatter_dimension=0, tiled=True
        ).astype(jnp.float32),
        lax.psum_scatter(
            grad_up.astype(jnp.bfloat16), "fsdp", scatter_dimension=0, tiled=True
        ).astype(jnp.float32),
        lax.psum_scatter(
            grad_down.astype(jnp.bfloat16), "fsdp", scatter_dimension=0, tiled=True
        ).astype(jnp.float32),
    )
    grad_low_one = grad_hidden_one.astype(jnp.bfloat16)
    grad_out_w = jnp.dot(attended_flat.T, grad_low_one, preferred_element_type=jnp.float32)
    attended_gradient = jnp.dot(
        grad_low_one, whole_out.T, preferred_element_type=jnp.float32
    ).astype(jnp.bfloat16)
    attended_gradient = attended_gradient.reshape(
        sequence_count, span_length, QUERY_HEADS * HEAD_DIM
    )
    grad_heads = lax.all_to_all(attended_gradient, "seq", split_axis=2, concat_axis=1, tiled=True)
    full_len = grad_heads.shape[1]
    full_cos, full_sin = rope_tables(jnp.arange(full_len, dtype=jnp.int32), HEAD_DIM)
    back_fn = partial(
        attend_back_item, group_size=group_size, head_size=HEAD_DIM, cosine=full_cos, sine=full_sin
    )
    packed_grads = lax.map(back_fn, (head_inputs, heads_attended, log_totals, grad_heads))
    token_gradients = lax.all_to_all(
        packed_grads, "seq", split_axis=1, concat_axis=2, tiled=True
    ).reshape(row_count, KEY_VALUE_HEADS, group_size + 2, HEAD_DIM)
    grad_queries = token_gradients[:, :, :group_size, :].reshape(row_count, QUERY_HEADS * HEAD_DIM)
    key_gradients = token_gradients[:, :, group_size, :].reshape(
        row_count, KEY_VALUE_HEADS * HEAD_DIM
    )
    value_gradients = token_gradients[:, :, group_size + 1, :].reshape(
        row_count, KEY_VALUE_HEADS * HEAD_DIM
    )
    grad_query = jnp.dot(first_inputs.T, grad_queries, preferred_element_type=jnp.float32)
    grad_key = jnp.dot(first_inputs.T, key_gradients, preferred_element_type=jnp.float32)
    grad_value = jnp.dot(first_inputs.T, value_gradients, preferred_element_type=jnp.float32)
    grad_inputs_one = (
        jnp.dot(grad_queries, whole_query.T, preferred_element_type=jnp.float32)
        + jnp.dot(key_gradients, whole_key.T, preferred_element_type=jnp.float32)
        + jnp.dot(value_gradients, whole_value.T, preferred_element_type=jnp.float32)
    )
    gain_grad_one = jnp.sum(grad_inputs_one * normed_one, axis=0)
    grad_tokens = grad_hidden_one + norm_back(grad_inputs_one, normed_one, inv_one, gain_one)
    attn_shards = (
        lax.psum_scatter(
            gain_grad_one.astype(jnp.bfloat16), "fsdp", scatter_dimension=0, tiled=True
        ).astype(jnp.float32),
        lax.psum_scatter(
            grad_query.astype(jnp.bfloat16), "fsdp", scatter_dimension=0, tiled=True
        ).astype(jnp.float32),
        lax.psum_scatter(
            grad_key.astype(jnp.bfloat16), "fsdp", scatter_dimension=0, tiled=True
        ).astype(jnp.float32),
        lax.psum_scatter(
            grad_value.astype(jnp.bfloat16), "fsdp", scatter_dimension=0, tiled=True
        ).astype(jnp.float32),
        lax.psum_scatter(
            grad_out_w.astype(jnp.bfloat16), "fsdp", scatter_dimension=0, tiled=True
        ).astype(jnp.float32),
    )
    summed = (
        lax.psum(attn_shards[0].astype(jnp.bfloat16), "seq").astype(jnp.float32),
        lax.psum(ffn_shards[0].astype(jnp.bfloat16), "seq").astype(jnp.float32),
        lax.psum(attn_shards[1].astype(jnp.bfloat16), "seq").astype(jnp.float32),
        lax.psum(attn_shards[2].astype(jnp.bfloat16), "seq").astype(jnp.float32),
        lax.psum(attn_shards[3].astype(jnp.bfloat16), "seq").astype(jnp.float32),
        lax.psum(attn_shards[4].astype(jnp.bfloat16), "seq").astype(jnp.float32),
        lax.psum(ffn_shards[1].astype(jnp.bfloat16), "seq").astype(jnp.float32),
        lax.psum(ffn_shards[2].astype(jnp.bfloat16), "seq").astype(jnp.float32),
        lax.psum(ffn_shards[3].astype(jnp.bfloat16), "seq").astype(jnp.float32),
    )
    return (
        block_out.reshape(sequence_count, span_length, width),
        grad_tokens.reshape(sequence_count, span_length, width),
        summed[0],
        summed[1],
        summed[2],
        summed[3],
        summed[4],
        summed[5],
        summed[6],
        summed[7],
        summed[8],
    )


def solution(mesh):
    placed = (
        P("fsdp", "seq", None),
        P("fsdp", "seq", None),
        P("fsdp"),
        P("fsdp"),
        P("fsdp", None),
        P("fsdp", None),
        P("fsdp", None),
        P("fsdp", None),
        P("fsdp", None),
        P("fsdp", None),
        P("fsdp", None),
    )
    return jax.shard_map(
        body,
        mesh=mesh,
        in_specs=placed,
        out_specs=(
            P("fsdp", "seq", None),
            P("fsdp", "seq", None),
            P("fsdp"),
            P("fsdp"),
            P("fsdp", None),
            P("fsdp", None),
            P("fsdp", None),
            P("fsdp", None),
            P("fsdp", None),
            P("fsdp", None),
            P("fsdp", None),
        ),
        check_vma=False,
    )
```

profile of v0, /device:TPU:0, one launch (start us, length us, event | category | flops | bytes accessed | tf_op | source)
XLA Modules:
  0.0 1337.4 jit_solution(4431075528565036426)
XLA Ops:
  13.8 15.5 %all-reduce.5 = (bf16[1536]{0:T(1024)(128)(2,1)S(1)}, bf16[1536]{0:T(1024)(128)(2,1)S(1)}) all-reduce(bf16[1536]{0:T(1024)(128)(2,1)S(1)} %dynamic-update-slice, bf16[1536]{0:T(1024)(128)(2,1)S(1)} %dynamic-update-slice.1), channel_id=1, replica_groups=mesh['seq'=4,'fsdp'=8] {'fsdp'}, use_global_device_ids=true, to_apply=%add | all-reduce | flops 3072 | bytes 12288
  33.0 8.7 all-gather.10.cloned.1.call-done
  44.6 4.0 fusion.45
  48.5 24.0 %all-gather.12.cloned.1.call-done = bf16[1536,768]{1,0:T(8,128)(2,1)} async-done(((bf16[192,768]{1,0:T(8,128)(2,1)}), bf16[1536,768]{1,0:T(8,128)(2,1)}) %all-gather.12.cloned.1.call-update) | async-done | bytes 2359312 | tf_op jit(solution)/shard_map/all_gather | solution.py:147
  72.5 3.5 convolution_convert_fusion.8
  78.4 34.8 %all-gather.8.cloned.1.call-done = bf16[1536,1536]{1,0:T(8,128)(2,1)} async-done(((bf16[192,1536]{1,0:T(8,128)(2,1)}), bf16[1536,1536]{1,0:T(8,128)(2,1)}) %all-gather.8.cloned.1.call-update) | async-done | bytes 4718608 | tf_op jit(solution)/shard_map/all_gather | solution.py:145
  113.2 6.8 copy.68
  120.1 4.6 fusion.44
  129.3 4.7 all-to-all-start
  134.1 71.1 %all-to-all-done = bf16[2,256,3072]{1,0,2:T(2,128)(2,1)S(1)} async-done(((bf16[2,256,3072]{1,0,2:T(2,128)(2,1)}), bf16[2,256,3072]{1,0,2:T(2,128)(2,1)S(1)}, u32[]{:S(2)}, u32[]{:S(2)}) %all-to-all-start) | async-done | bytes 3145760 | tf_op jit(solution)/shard_map/all_to_all | solution.py:192
  207.2 4.6 copy.74
  215.1 29.1 %while.25 = (s32[]{:T(128)}, bf16[2,1024,384]{1,2,0:T(8,128)(2,1)}, f32[2,2,2,1024]{3,2,1,0:T(2,128)S(1)}, bf16[2,1024,768]{1,2,0:T(8,128)(2,1)S(1)}, s32[]{:T(128)}) while((s32[]{:T(128)}, bf16[2,1024,384]{1,2,0:T(8,128)(2,1)}, f32[2,2,2,1024]{3,2,1,0:T(2,128)S(1)}, bf16[2,1024,768]{1,2,0:T(8,128)(2,1)S(1)}, s32[]{:T(128)}) %tuple.80), condition=%wide.region_4.5_spmd, body=%wide.region_1.4_spmd.sunk | while | flops 1658187776 | bytes 68026976 | solution.py:77
  215.5 3.4 fusion.109
  219.0 3.7 exponential_reduce_fusion.2
  222.7 5.9 fusion.110
  230.0 3.4 fusion.109
  233.5 3.7 exponential_reduce_fusion.2
  237.2 6.0 fusion.110
  244.1 4.9 copy.76
  249.1 4.6 all-to-all-start.1
  256.9 33.5 %all-to-all-done.1 = bf16[2,1024,384]{2,0,1:T(2,128)(2,1)} async-done(((bf16[2,1024,384]{2,0,1:T(2,128)(2,1)}), bf16[2,1024,384]{2,0,1:T(2,128)(2,1)}, u32[]{:S(2)}, u32[]{:S(2)}) %all-to-all-start.1) | async-done | bytes 1572896 | tf_op jit(solution)/shard_map/all_to_all | solution.py:194
  294.4 6.5 multiply_reduce_fusion.4
  304.1 12.1 fusion.46
  316.2 12.2 fusion.47
  328.4 46.9 %all-gather.20.cloned.1.call-done = bf16[4096,1536]{1,0:T(8,128)(2,1)} async-done(((bf16[512,1536]{1,0:T(8,128)(2,1)}), bf16[4096,1536]{1,0:T(8,128)(2,1)}) %all-gather.20.cloned.1.call-update) | async-done | bytes 12582928 | tf_op jit(solution)/shard_map/all_gather | solution.py:213
  375.2 19.2 %multiply_convert_fusion = (bf16[512,4096]{1,0:T(8,128)(2,1)}, bf16[512,4096]{1,0:T(8,128)(2,1)}, bf16[512,4096]{1,0:T(8,128)(2,1)}) fusion(f32[512,4096]{1,0:T(8,128)} %fusion.46, f32[512,4096]{1,0:T(8,128)} %fusion.47, bf16[512,1536]{1,0:T(8,128)(2,1)} %bitcast_convert_fusion, bf16[4096,1536]{1,0:T(8,128)(2,1)} %all-gather.20.cloned.1.call-done), kind=kOutput, calls=%fused_computation.61 | convolution fusion | flops 6476005376 | bytes 43515904 | tf_op jit(solution)/shard_map/dot_general | solution.py:220
  394.4 11.2 fusion.48
  405.7 12.0 multiply_reduce_fusion
  418.4 7.3 convolution_convert_fusion.7
  425.7 4.9 copy.78
  430.6 4.6 all-to-all-start.2
  435.2 7.1 convolution_convert_fusion.3
  442.4 30.3 %all-to-all-done.2 = bf16[2,256,1536]{1,0,2:T(2,128)(2,1)} async-done(((bf16[2,256,1536]{1,0,2:T(2,128)(2,1)}), bf16[2,256,1536]{1,0,2:T(2,128)(2,1)}, u32[]{:S(2)}, u32[]{:S(2)}) %all-to-all-start.2) | async-done | bytes 1572896 | tf_op jit(solution)/shard_map/all_to_all | solution.py:262
  472.6 3.8 copy.79
  476.5 3.8 all_to_all.58
  480.3 73.4 %while.26 = (s32[]{:T(128)}, bf16[2,1024,768]{1,2,0:T(8,128)(2,1)}, bf16[2,1024,768]{1,2,0:T(8,128)(2,1)S(1)}, f32[2,2,2,1024]{3,2,1,0:T(2,128)S(1)}, bf16[2,102...) while((s32[]{:T(128)}, bf16[2,1024,768]{1,2,0:T(8,128)(2,1)}, ...), condition=%wide.region_8.9_spmd.clone.clone.clone, body=%wide.region_7.8_spmd.clone.clone.clone.sunk | while | flops 4085755904 | bytes 115446648 | solution.py:268
  482.4 8.3 fusion.118
  491.0 10.1 fusion.121
  507.3 8.3 fusion.119
  518.9 8.1 fusion.118
  527.4 10.0 fusion.121
  543.6 8.3 fusion.119
  553.6 7.6 copy.81
  561.3 73.6 %all_to_all.66 = bf16[2,1024,768]{2,0,1:T(2,128)(2,1)} all-to-all(bf16[2,1024,768]{2,0,1:T(2,128)(2,1)S(1)} %copy.81), channel_id=1, replica_groups=mesh['seq'=4,'fsdp'=8] {'seq'}, dimensions={1} | all-to-all | bytes 6291456 | tf_op jit(solution)/shard_map/all_to_all | solution.py:269
  634.9 11.2 copy.82
  646.0 4.6 reshape.351
  655.4 4.5 convolution_convert_fusion.5
  662.1 4.4 convolution_convert_fusion.4
  667.9 11.8 convolution_convert_fusion.2
  679.8 11.9 convolution_convert_fusion.1
  693.1 11.9 convolution_convert_fusion
  705.1 37.1 %reduce-scatter.12.cloned.1.call-done = bf16[192,768]{1,0:T(8,128)(2,1)} async-done(((bf16[1536,768]{1,0:T(8,128)(2,1)}), bf16[192,768]{1,0:T(8,128)(2,1)}) %reduce-scatter.12.cloned.1.call-update) | async-done | bytes 294928 | tf_op jit(solution)/shard_map/reduce_scatter | solution.py:299
  742.2 57.3 %reduce-scatter.8.cloned.1.call-done = bf16[192,1536]{1,0:T(8,128)(2,1)} async-done(((bf16[1536,1536]{1,0:T(8,128)(2,1)}), bf16[192,1536]{1,0:T(8,128)(2,1)}) %reduce-scatter.8.cloned.1.call-update) | async-done | bytes 589840 | tf_op jit(solution)/shard_map/reduce_scatter | solution.py:293
  799.5 95.7 %reduce-scatter.16.cloned.1.call-done = bf16[192,4096]{1,0:T(8,128)(2,1)} async-done(((bf16[1536,4096]{1,0:T(8,128)(2,1)}), bf16[192,4096]{1,0:T(8,128)(2,1)}) %reduce-scatter.16.cloned.1.call-update) | async-done | bytes 1572880 | tf_op jit(solution)/shard_map/reduce_scatter | solution.py:244
  895.2 95.8 %reduce-scatter.18.cloned.1.call-done = bf16[192,4096]{1,0:T(8,128)(2,1)} async-done(((bf16[1536,4096]{1,0:T(8,128)(2,1)}), bf16[192,4096]{1,0:T(8,128)(2,1)}) %reduce-scatter.18.cloned.1.call-update) | async-done | bytes 1572880 | tf_op jit(solution)/shard_map/reduce_scatter | solution.py:247
  991.0 95.7 %reduce-scatter.20.cloned.1.call-done = bf16[512,1536]{1,0:T(8,128)(2,1)} async-done(((bf16[4096,1536]{1,0:T(8,128)(2,1)}), bf16[512,1536]{1,0:T(8,128)(2,1)}) %reduce-scatter.20.cloned.1.call-update) | async-done | bytes 1572880 | tf_op jit(solution)/shard_map/reduce_scatter | solution.py:250
  1088.5 12.2 convolution_add_fusion.3
  1100.8 4.7 fusion.49
  1108.4 3.7 multiply_reduce_fusion.1
  1112.1 13.6 %all-reduce.4 = (bf16[1536]{0:T(1024)(128)(2,1)S(1)}, bf16[1536]{0:T(1024)(128)(2,1)S(1)}) all-reduce(bf16[1536]{0:T(1024)(128)(2,1)S(1)} %get-tuple-element.208, bf16[1536]{0:T(1024)(128)(2,1)S(1)} %copy-done.38), channel_id=2, replica_groups=mesh['seq'=4,'fsdp'=8] {'fsdp'}, use_global_device_ids=true, to_apply=%region_11.12.clone | all-reduce | flops 3072 | bytes 12288
  1125.8 12.3 all-reduce.6
  1139.2 5.3 multiply_add_fusion
  1144.5 174.5 %all-reduce.10.cloned.1.call-done = (bf16[192,1536]{1,0:T(8,128)(2,1)}, bf16[192,768]{1,0:T(8,128)(2,1)}, bf16[192,768]{1,0:T(8,128)(2,1)}, bf16[192,1536]{1,0:T...) async-done(((bf16[192,1536]{1,0:T(8,128)(2,1)}, bf16[192,768]{1,0:T(8,128)(2,1)}, bf16[192,768]{1,0:T(8,128)(2,1)}, ...) | async-done | bytes 6488080 | tf_op jit(solution)/shard_map/psum | solution.py:309
  1319.1 3.5 convert_element_type.210
  (213 shorter events, 81.3 us)
Async XLA Ops:
  7.2 34.6 %all-gather.10.cloned.1.call-start = ((), (), s32[]{:S(2)}) async-start(), calls=%async_computation.12 | async-start | bytes 2654208 | tf_op jit(solution)/shard_map/all_gather | solution.py:146
  7.9 4.1 copy-start.39
  7.9 5.4 copy-start.40
  7.9 5.6 copy-start.41
  7.9 21.4 %copy-start = (f32[2,256,1536]{2,1,0:T(8,128)S(1)}, f32[2,256,1536]{2,1,0:T(8,128)}, u32[]{:S(2)}) copy-start(f32[2,256,1536]{2,1,0:T(8,128)} %param.15) | copy-start | bytes 9437188
  8.0 64.6 %all-gather.12.cloned.1.call-start = ((), (), s32[]{:S(2)}) async-start(), calls=%async_computation.13 | async-start | bytes 2654208 | tf_op jit(solution)/shard_map/all_gather | solution.py:147
  8.7 104.5 %all-gather.8.cloned.1.call-start = ((), (), s32[]{:S(2)}) async-start(), calls=%async_computation.11 | async-start | bytes 5308416 | tf_op jit(solution)/shard_map/all_gather | solution.py:145
  9.4 285.0 %all-gather.14.cloned.1.call-start = ((), (), s32[]{:S(2)}) async-start(), calls=%async_computation.14 | async-start | bytes 5308416 | tf_op jit(solution)/shard_map/all_gather | solution.py:148
  10.0 294.1 %all-gather.16.cloned.1.call-start = ((), (), s32[]{:S(2)}) async-start(), calls=%async_computation.15 | async-start | bytes 14155776 | tf_op jit(solution)/shard_map/all_gather | solution.py:202
  10.6 305.6 %all-gather.18.cloned.1.call-start = ((), (), s32[]{:S(2)}) async-start(), calls=%async_computation.16 | async-start | bytes 14155776 | tf_op jit(solution)/shard_map/all_gather | solution.py:203
  11.2 364.1 %all-gather.20.cloned.1.call-start = ((), (), s32[]{:S(2)}) async-start(), calls=%async_computation.17 | async-start | bytes 14155776 | tf_op jit(solution)/shard_map/all_gather | solution.py:213
  12.0 18.0 %copy-start.36 = (f32[48]{0:T(128)}, f32[48]{0:T(128)S(1)}, u32[]{:S(2)}) copy-start(f32[48]{0:T(128)S(1)} %multiply_power_fusion) | copy-start | bytes 580
  29.3 2.2 copy-start.32
  30.1 1.5 copy-start.34
  48.5 28.7 %copy-start.20 = (f32[512,8,96]{0,2,1:T(8,128)S(1)}, f32[512,8,96]{0,2,1:T(8,128)}, u32[]{:S(2)}) copy-start(f32[512,8,96]{0,2,1:T(8,128)} %fusion.45) | copy-start | bytes 4718596
  113.2 6.8 copy-start.21
  124.7 1.1 copy-start.12
  124.7 1.4 copy-start.13
  129.3 75.8 %all-to-all-start = ((bf16[2,256,3072]{1,0,2:T(2,128)(2,1)}), bf16[2,256,3072]{1,0,2:T(2,128)(2,1)S(1)}, u32[]{:S(2)}, u32[]{:S(2)}) async-start(bf16[2,256,3072]{1,0,2:T(2,128)(2,1)} %reshape.346), calls=%async_computation | async-start | bytes 6291456 | tf_op jit(solution)/shard_map/all_to_all | solution.py:192
  215.2 3.8 copy-start.2
  229.7 3.8 copy-start.2
  249.1 41.3 %all-to-all-start.1 = ((bf16[2,1024,384]{2,0,1:T(2,128)(2,1)}), bf16[2,1024,384]{2,0,1:T(2,128)(2,1)}, u32[]{:S(2)}, u32[]{:S(2)}) async-start(bf16[2,1024,384]{2,0,1:T(2,128)(2,1)} %copy.76), calls=%async_computation.1 | async-start | bytes 3145728 | tf_op jit(solution)/shard_map/all_to_all | solution.py:194
  301.0 1.7 copy-start.8
  394.4 11.2 copy-start.9
  405.6 12.0 copy-start.6
  418.4 7.3 copy-start.7
  430.6 42.1 %all-to-all-start.2 = ((bf16[2,256,1536]{1,0,2:T(2,128)(2,1)}), bf16[2,256,1536]{1,0,2:T(2,128)(2,1)}, u32[]{:S(2)}, u32[]{:S(2)}) async-start(bf16[2,256,1536]{1,0,2:T(2,128)(2,1)} %copy.78), calls=%async_computation.2 | async-start | bytes 3145728 | tf_op jit(solution)/shard_map/all_to_all | solution.py:262
  435.2 270.0 %reduce-scatter.14.cloned.1.call-start = ((), (), s32[]{:S(2)}) async-start(), calls=%async_computation.21 | async-start | bytes 5308416 | tf_op jit(solution)/shard_map/reduce_scatter | solution.py:302
  442.3 262.8 %reduce-scatter.10.cloned.1.call-start = ((), (), s32[]{:S(2)}) async-start(), calls=%async_computation.19 | async-start | bytes 2654208 | tf_op jit(solution)/shard_map/reduce_scatter | solution.py:296
  472.6 7.6 copy-start.37
  491.0 10.2 copy-start.4
  504.4 2.9 copy-start.5
  507.3 8.3 copy-start.3
  527.4 10.0 copy-start.4
  540.7 2.9 copy-start.5
  543.6 8.3 copy-start.3
  650.6 1.9 copy-start.22
  651.6 0.9 copy-start.15
  655.4 86.8 %reduce-scatter.12.cloned.1.call-start = ((), (), s32[]{:S(2)}) async-start(), calls=%async_computation.20 | async-start | bytes 2654208 | tf_op jit(solution)/shard_map/reduce_scatter | solution.py:299
  659.9 139.6 %reduce-scatter.8.cloned.1.call-start = ((), (), s32[]{:S(2)}) async-start(), calls=%async_computation.18 | async-start | bytes 5308416 | tf_op jit(solution)/shard_map/reduce_scatter | solution.py:293
  660.0 2.1 copy-start.23
  660.1 1.1 copy-start.18
  666.5 1.4 copy-start.25
  666.5 228.7 %reduce-scatter.16.cloned.1.call-start = ((), (), s32[]{:S(2)}) async-start(), calls=%async_computation.22 | async-start | bytes 14155776 | tf_op jit(solution)/shard_map/reduce_scatter | solution.py:244
  679.8 311.2 %reduce-scatter.18.cloned.1.call-start = ((), (), s32[]{:S(2)}) async-start(), calls=%async_computation.23 | async-start | bytes 14155776 | tf_op jit(solution)/shard_map/reduce_scatter | solution.py:247
  691.7 1.4 copy-start.24
  691.7 394.9 %reduce-scatter.20.cloned.1.call-start = ((), (), s32[]{:S(2)}) async-start(), calls=%async_computation.24 | async-start | bytes 14155776 | tf_op jit(solution)/shard_map/reduce_scatter | solution.py:250
  705.0 614.0 %all-reduce.10.cloned.1.call-start = ((), (), s32[]{:S(2)}) async-start(), calls=%async_computation.25 | async-start | bytes 12976128 | tf_op jit(solution)/shard_map/psum | solution.py:309
  1086.6 1.9 copy-start.10
  1088.5 12.2 copy-start.19
  1100.8 4.7 copy-start.11
  1100.8 4.7 copy-start.16
  1105.5 1.9 copy-start.1
  1105.6 2.1 copy-start.14
  1105.6 2.8 copy-start.17
  1105.6 2.8 copy-start.33
  1105.6 2.8 copy-start.35
  1108.4 3.7 copy-start.38
  1319.1 3.6 copy-start.27
  1322.6 2.0 copy-start.26
  1324.6 2.1 copy-start.29
  1324.6 3.2 copy-start.28
  1324.6 4.4 copy-start.31
  1326.7 3.2 copy-start.30
Sparse Core Ops, SparseCore 0:
  9.9 31.8 all-gather.9
  43.6 28.8 all-gather.11
  74.4 38.7 all-gather.7
  115.0 38.7 all-gather.13
  155.5 71.9 all-gather.15
  229.3 71.9 all-gather.17
  303.2 71.9 all-gather.19
  442.5 54.2 reduce-scatter.13
  655.5 40.4 reduce-scatter.9
  699.8 42.3 reduce-scatter.11
  745.7 53.7 reduce-scatter.7
  802.8 92.2 reduce-scatter.15
  898.7 92.2 reduce-scatter.17
  994.3 92.2 reduce-scatter.19
  1089.4 229.5 all-reduce.9
where the time goes:
time: 1340 us
  waiting for transfers between devices  810 us (60%)
  matrix products  249 us (19%)
  blocking collectives  115 us (9%)
  local copies, waits for them, and re-layouts  89.6 us (7%)
  other arithmetic  42.4 us (3%)
  between operations  16.2 us (1%)
  starting transfers between devices  14.4 us (1%)
    psum x1, waiting for transfers between devices, body(): lax.psum(attn_shards[1].astype(jnp.bfloat16), 'seq').astype(jnp.float32)  175 us
    reduce_scatter x1, waiting for transfers between devices, body(): lax.psum_scatter(grad_up.astype(jnp.bfloat16), 'fsdp', scatter_dimension=...  95.8 us
    reduce_scatter x1, waiting for transfers between devices, body(): lax.psum_scatter(grad_gate.astype(jnp.bfloat16), 'fsdp', scatter_dimensio...  95.7 us
    reduce_scatter x1, waiting for transfers between devices, body(): lax.psum_scatter(grad_down.astype(jnp.bfloat16), 'fsdp', scatter_dimensio...  95.7 us
    all_to_all x1, blocking collectives, body(): lax.all_to_all(packed_grads, 'seq', split_axis=1, concat_axis=2, tiled=True)  73.6 us
    all_to_all x1, waiting for transfers between devices, body(): lax.all_to_all(packed_arrays, 'seq', split_axis=2, concat_axis=1, tiled=T...  71.1 us
    reduce_scatter x1, waiting for transfers between devices, body(): lax.psum_scatter(grad_query.astype(jnp.bfloat16), 'fsdp', scatter_dimensi...  57.3 us
    all_gather x1, waiting for transfers between devices, body(): lax.all_gather(down_weight, 'fsdp', axis=0, tiled=True)  46.9 us
  transfers between devices with their start and end apart: 18, of which 13 were waited for; matrix products, arithmetic and copies ran while one was open for 22% of the time, Pallas kernels for 0%

commit v1 on v0

--- a/solution.py
+++ b/solution.py
@@ -306,7 +306,9 @@
     summed = (
         lax.psum(attn_shards[0].astype(jnp.bfloat16), "seq").astype(jnp.float32),
         lax.psum(ffn_shards[0].astype(jnp.bfloat16), "seq").astype(jnp.float32),
-        lax.psum(attn_shards[1].astype(jnp.bfloat16), "seq").astype(jnp.float32),
+        jnp.sum(lax.all_gather(attn_shards[1].astype(jnp.bfloat16), "seq"), axis=0).astype(
+            jnp.float32
+        ),
         lax.psum(attn_shards[2].astype(jnp.bfloat16), "seq").astype(jnp.float32),
         lax.psum(attn_shards[3].astype(jnp.bfloat16), "seq").astype(jnp.float32),
         lax.psum(attn_shards[4].astype(jnp.bfloat16), "seq").astype(jnp.float32),

time: 1340 us -> 1430 us (1.067)
  waiting for transfers between devices: 810 us -> 899 us
    reduce_scatter x1, waiting for transfers between devices: 57.3 us -> 0.02 us  [body(): lax.psum_scatter(grad_query.astype(jnp.bfloat16), 'fsdp', scatter_dimensi...]
    reduce_scatter x1, waiting for transfers between devices: 0.02 us -> 54.6 us  [body(): lax.psum_scatter(grad_out_w.astype(jnp.bfloat16), 'fsdp', scatter_dimensi...]
    reduce_scatter x1, waiting for transfers between devices: 0.02 us -> 46.1 us  [body(): lax.psum_scatter(grad_key.astype(jnp.bfloat16), 'fsdp', scatter_dimension...]
    psum x1, waiting for transfers between devices: 175 us -> 203 us  [body(): lax.psum(attn_shards[2].astype(jnp.bfloat16), 'seq').astype(jnp.float32)]
  transfers between devices with their start and end apart: 18 -> 19, of which waited for: 13 -> 14; matrix products, arithmetic and copies ran while one was open for 22% -> 14% of each run, Pallas kernels for 0% -> 0%
where the time goes in v1:
time: 1430 us
  waiting for transfers between devices  899 us (63%)
  matrix products  248 us (17%)
  blocking collectives  115 us (8%)
  local copies, waits for them, and re-layouts  88.4 us (6%)
  other arithmetic  44.6 us (3%)
  between operations  16.2 us (1%)
  starting transfers between devices  14.7 us (1%)
    psum x1, waiting for transfers between devices, body(): lax.psum(attn_shards[2].astype(jnp.bfloat16), 'seq').astype(jnp.float32)  203 us
    reduce_scatter x1, waiting for transfers between devices, body(): lax.psum_scatter(grad_up.astype(jnp.bfloat16), 'fsdp', scatter_dimension=...  95.8 us
    reduce_scatter x1, waiting for transfers between devices, body(): lax.psum_scatter(grad_gate.astype(jnp.bfloat16), 'fsdp', scatter_dimensio...  95.7 us
    reduce_scatter x1, waiting for transfers between devices, body(): lax.psum_scatter(grad_down.astype(jnp.bfloat16), 'fsdp', scatter_dimensio...  95.7 us
    all_to_all x1, blocking collectives, body(): lax.all_to_all(packed_grads, 'seq', split_axis=1, concat_axis=2, tiled=True)  73.6 us
    all_to_all x1, waiting for transfers between devices, body(): lax.all_to_all(packed_arrays, 'seq', split_axis=2, concat_axis=1, tiled=T...  71.1 us
    reduce_scatter x1, waiting for transfers between devices, body(): lax.psum_scatter(grad_out_w.astype(jnp.bfloat16), 'fsdp', scatter_dimensi...  54.6 us
    all_gather x1, waiting for transfers between devices, body(): lax.all_gather(down_weight, 'fsdp', axis=0, tiled=True)  46.8 us
  transfers between devices with their start and end apart: 19, of which 14 were waited for; matrix products, arithmetic and copies ran while one was open for 14% of the time, Pallas kernels for 0%

profile of v1, /device:TPU:0, one launch (start us, length us, event | category | flops | bytes accessed | tf_op | source)
XLA Modules:
  0.0 1426.6 jit_solution(10523342368372629418)
XLA Ops:
  13.8 15.5 %all-reduce.5 = (bf16[1536]{0:T(1024)(128)(2,1)S(1)}, bf16[1536]{0:T(1024)(128)(2,1)S(1)}) all-reduce(bf16[1536]{0:T(1024)(128)(2,1)S(1)} %dynamic-update-slice, bf16[1536]{0:T(1024)(128)(2,1)S(1)} %dynamic-update-slice.1), channel_id=1, replica_groups=mesh['seq'=4,'fsdp'=8] {'fsdp'}, use_global_device_ids=true, to_apply=%add | all-reduce | flops 3072 | bytes 12288
  33.0 8.7 all-gather.12.cloned.1.call-done
  44.6 4.0 fusion.45
  48.5 24.0 %all-gather.14.cloned.1.call-done = bf16[1536,768]{1,0:T(8,128)(2,1)} async-done(((bf16[192,768]{1,0:T(8,128)(2,1)}), bf16[1536,768]{1,0:T(8,128)(2,1)}) %all-gather.14.cloned.1.call-update) | async-done | bytes 2359312 | tf_op jit(solution)/shard_map/all_gather | solution.py:147
  72.5 3.5 convolution_convert_fusion.8
  78.4 34.8 %all-gather.10.cloned.1.call-done = bf16[1536,1536]{1,0:T(8,128)(2,1)} async-done(((bf16[192,1536]{1,0:T(8,128)(2,1)}), bf16[1536,1536]{1,0:T(8,128)(2,1)}) %all-gather.10.cloned.1.call-update) | async-done | bytes 4718608 | tf_op jit(solution)/shard_map/all_gather | solution.py:145
  113.2 6.8 copy.68
  120.1 4.6 fusion.44
  129.3 5.0 all-to-all-start
  134.3 71.1 %all-to-all-done = bf16[2,256,3072]{1,0,2:T(2,128)(2,1)S(1)} async-done(((bf16[2,256,3072]{1,0,2:T(2,128)(2,1)}), bf16[2,256,3072]{1,0,2:T(2,128)(2,1)S(1)}, u32[]{:S(2)}, u32[]{:S(2)}) %all-to-all-start) | async-done | bytes 3145760 | tf_op jit(solution)/shard_map/all_to_all | solution.py:192
  207.5 4.6 copy.74
  215.3 29.1 %while.25 = (s32[]{:T(128)}, bf16[2,1024,384]{1,2,0:T(8,128)(2,1)}, f32[2,2,2,1024]{3,2,1,0:T(2,128)S(1)}, bf16[2,1024,768]{1,2,0:T(8,128)(2,1)S(1)}, s32[]{:T(128)}) while((s32[]{:T(128)}, bf16[2,1024,384]{1,2,0:T(8,128)(2,1)}, f32[2,2,2,1024]{3,2,1,0:T(2,128)S(1)}, bf16[2,1024,768]{1,2,0:T(8,128)(2,1)S(1)}, s32[]{:T(128)}) %tuple.80), condition=%wide.region_4.5_spmd, body=%wide.region_1.4_spmd.sunk | while | flops 1658187776 | bytes 68026976 | solution.py:77
  215.8 3.4 fusion.109
  219.2 3.7 exponential_reduce_fusion.2
  222.9 5.9 fusion.110
  230.3 3.4 fusion.109
  233.7 3.7 exponential_reduce_fusion.2
  237.4 6.0 fusion.110
  244.4 4.9 copy.76
  249.3 4.5 all-to-all-start.1
  257.1 33.4 %all-to-all-done.1 = bf16[2,1024,384]{2,0,1:T(2,128)(2,1)} async-done(((bf16[2,1024,384]{2,0,1:T(2,128)(2,1)}), bf16[2,1024,384]{2,0,1:T(2,128)(2,1)}, u32[]{:S(2)}, u32[]{:S(2)}) %all-to-all-start.1) | async-done | bytes 1572896 | tf_op jit(solution)/shard_map/all_to_all | solution.py:194
  294.5 6.5 multiply_reduce_fusion.4
  304.2 12.2 fusion.46
  316.4 12.1 fusion.47
  328.5 46.8 %all-gather.22.cloned.1.call-done = bf16[4096,1536]{1,0:T(8,128)(2,1)} async-done(((bf16[512,1536]{1,0:T(8,128)(2,1)}), bf16[4096,1536]{1,0:T(8,128)(2,1)}) %all-gather.22.cloned.1.call-update) | async-done | bytes 12582928 | tf_op jit(solution)/shard_map/all_gather | solution.py:213
  375.3 19.2 %multiply_convert_fusion = (bf16[512,4096]{1,0:T(8,128)(2,1)}, bf16[512,4096]{1,0:T(8,128)(2,1)}, bf16[512,4096]{1,0:T(8,128)(2,1)}) fusion(f32[512,4096]{1,0:T(8,128)} %fusion.46, f32[512,4096]{1,0:T(8,128)} %fusion.47, bf16[512,1536]{1,0:T(8,128)(2,1)} %bitcast_convert_fusion, bf16[4096,1536]{1,0:T(8,128)(2,1)} %all-gather.22.cloned.1.call-done), kind=kOutput, calls=%fused_computation.61 | convolution fusion | flops 6476005376 | bytes 43515904 | tf_op jit(solution)/shard_map/dot_general | solution.py:220
  394.5 10.9 fusion.48
  405.5 12.0 multiply_reduce_fusion
  418.2 7.3 convolution_convert_fusion.7
  425.5 4.9 copy.78
  430.4 4.6 all-to-all-start.2
  435.0 37.5 %all-to-all-done.2 = bf16[2,256,1536]{1,0,2:T(2,128)(2,1)} async-done(((bf16[2,256,1536]{1,0,2:T(2,128)(2,1)}), bf16[2,256,1536]{1,0,2:T(2,128)(2,1)}, u32[]{:S(2)}, u32[]{:S(2)}) %all-to-all-start.2) | async-done | bytes 1572896 | tf_op jit(solution)/shard_map/all_to_all | solution.py:262
  472.5 3.9 copy.79
  476.4 3.8 all_to_all.58
  480.1 73.1 %while.26 = (s32[]{:T(128)}, bf16[2,1024,768]{1,2,0:T(8,128)(2,1)}, bf16[2,1024,768]{1,2,0:T(8,128)(2,1)S(1)}, f32[2,2,2,1024]{3,2,1,0:T(2,128)S(1)}, bf16[2,102...) while((s32[]{:T(128)}, bf16[2,1024,768]{1,2,0:T(8,128)(2,1)}, ...), condition=%wide.region_8.9_spmd.clone.clone.clone, body=%wide.region_7.8_spmd.clone.clone.clone.sunk | while | flops 4085755904 | bytes 115446648 | solution.py:268
  482.5 8.2 fusion.118
  491.0 10.0 fusion.121
  507.2 8.3 fusion.119
  518.8 8.2 fusion.118
  527.2 10.0 fusion.121
  543.5 8.3 fusion.119
  553.3 7.6 copy.81
  560.9 73.6 %all_to_all.66 = bf16[2,1024,768]{2,0,1:T(2,128)(2,1)} all-to-all(bf16[2,1024,768]{2,0,1:T(2,128)(2,1)S(1)} %copy.81), channel_id=1, replica_groups=mesh['seq'=4,'fsdp'=8] {'seq'}, dimensions={1} | all-to-all | bytes 6291456 | tf_op jit(solution)/shard_map/all_to_all | solution.py:269
  634.5 11.2 copy.82
  645.7 4.6 reshape.351
  652.3 4.4 convolution_convert_fusion.4
  656.8 7.3 convolution_convert_fusion.3
  671.9 11.7 convolution_convert_fusion.2
  685.1 12.0 convolution_convert_fusion.1
  698.5 12.3 convolution_convert_fusion
  711.5 54.6 %reduce-scatter.14.cloned.1.call-done = bf16[192,1536]{1,0:T(8,128)(2,1)} async-done(((bf16[1536,1536]{1,0:T(8,128)(2,1)}), bf16[192,1536]{1,0:T(8,128)(2,1)}) %reduce-scatter.14.cloned.1.call-update) | async-done | bytes 589840 | tf_op jit(solution)/shard_map/reduce_scatter | solution.py:302
  766.1 46.1 %reduce-scatter.10.cloned.1.call-done = bf16[192,768]{1,0:T(8,128)(2,1)} async-done(((bf16[1536,768]{1,0:T(8,128)(2,1)}), bf16[192,768]{1,0:T(8,128)(2,1)}) %reduce-scatter.10.cloned.1.call-update) | async-done | bytes 294928 | tf_op jit(solution)/shard_map/reduce_scatter | solution.py:296
  812.2 46.3 %reduce-scatter.12.cloned.1.call-done = bf16[192,768]{1,0:T(8,128)(2,1)} async-done(((bf16[1536,768]{1,0:T(8,128)(2,1)}), bf16[192,768]{1,0:T(8,128)(2,1)}) %reduce-scatter.12.cloned.1.call-update) | async-done | bytes 294928 | tf_op jit(solution)/shard_map/reduce_scatter | solution.py:299
  858.5 95.7 %reduce-scatter.16.cloned.1.call-done = bf16[192,4096]{1,0:T(8,128)(2,1)} async-done(((bf16[1536,4096]{1,0:T(8,128)(2,1)}), bf16[192,4096]{1,0:T(8,128)(2,1)}) %reduce-scatter.16.cloned.1.call-update) | async-done | bytes 1572880 | tf_op jit(solution)/shard_map/reduce_scatter | solution.py:244
  954.2 95.8 %reduce-scatter.18.cloned.1.call-done = bf16[192,4096]{1,0:T(8,128)(2,1)} async-done(((bf16[1536,4096]{1,0:T(8,128)(2,1)}), bf16[192,4096]{1,0:T(8,128)(2,1)}) %reduce-scatter.18.cloned.1.call-update) | async-done | bytes 1572880 | tf_op jit(solution)/shard_map/reduce_scatter | solution.py:247
  1050.0 95.7 %reduce-scatter.20.cloned.1.call-done = bf16[512,1536]{1,0:T(8,128)(2,1)} async-done(((bf16[4096,1536]{1,0:T(8,128)(2,1)}), bf16[512,1536]{1,0:T(8,128)(2,1)}) %reduce-scatter.20.cloned.1.call-update) | async-done | bytes 1572880 | tf_op jit(solution)/shard_map/reduce_scatter | solution.py:250
  1146.3 12.4 convolution_add_fusion.3
  1158.7 4.7 fusion.49
  1166.3 3.7 multiply_reduce_fusion.1
  1170.0 13.6 all-reduce.4
  1183.8 12.2 all-reduce.6
  1197.1 5.2 multiply_add_fusion
  1205.7 203.4 %all-reduce.10.cloned.1.call-done = (bf16[192,768]{1,0:T(8,128)(2,1)}, bf16[192,768]{1,0:T(8,128)(2,1)}, bf16[192,1536]{1,0:T(8,128)(2,1)}, bf16[192,4096]{1,0:T...) async-done(((bf16[192,768]{1,0:T(8,128)(2,1)}, bf16[192,768]{1,0:T(8,128)(2,1)}, bf16[192,1536]{1,0:T(8,128)(2,1)}, bf16[192,4096]{1,0:T(8,128)(2,1)}, ...) | async-done | bytes 5898256 | tf_op jit(solution)/shard_map/psum | solution.py:312
  1409.1 3.5 convert_element_type.212
  (219 shorter events, 85.7 us)
Async XLA Ops:
  7.2 34.6 %all-gather.12.cloned.1.call-start = ((), (), s32[]{:S(2)}) async-start(), calls=%async_computation.12 | async-start | bytes 2654208 | tf_op jit(solution)/shard_map/all_gather | solution.py:146
  7.9 4.1 copy-start.40
  7.9 5.3 copy-start.41
  7.9 5.6 copy-start.42
  7.9 21.4 %copy-start = (f32[2,256,1536]{2,1,0:T(8,128)S(1)}, f32[2,256,1536]{2,1,0:T(8,128)}, u32[]{:S(2)}) copy-start(f32[2,256,1536]{2,1,0:T(8,128)} %param.15) | copy-start | bytes 9437188
  8.0 64.6 %all-gather.14.cloned.1.call-start = ((), (), s32[]{:S(2)}) async-start(), calls=%async_computation.13 | async-start | bytes 2654208 | tf_op jit(solution)/shard_map/all_gather | solution.py:147
  8.7 104.5 %all-gather.10.cloned.1.call-start = ((), (), s32[]{:S(2)}) async-start(), calls=%async_computation.11 | async-start | bytes 5308416 | tf_op jit(solution)/shard_map/all_gather | solution.py:145
  9.4 285.1 %all-gather.16.cloned.1.call-start = ((), (), s32[]{:S(2)}) async-start(), calls=%async_computation.14 | async-start | bytes 5308416 | tf_op jit(solution)/shard_map/all_gather | solution.py:148
  10.0 294.2 %all-gather.18.cloned.1.call-start = ((), (), s32[]{:S(2)}) async-start(), calls=%async_computation.15 | async-start | bytes 14155776 | tf_op jit(solution)/shard_map/all_gather | solution.py:202
  10.6 305.8 %all-gather.20.cloned.1.call-start = ((), (), s32[]{:S(2)}) async-start(), calls=%async_computation.16 | async-start | bytes 14155776 | tf_op jit(solution)/shard_map/all_gather | solution.py:203
  11.2 364.1 %all-gather.22.cloned.1.call-start = ((), (), s32[]{:S(2)}) async-start(), calls=%async_computation.17 | async-start | bytes 14155776 | tf_op jit(solution)/shard_map/all_gather | solution.py:213
  12.0 18.0 %copy-start.37 = (f32[48]{0:T(128)}, f32[48]{0:T(128)S(1)}, u32[]{:S(2)}) copy-start(f32[48]{0:T(128)S(1)} %multiply_power_fusion) | copy-start | bytes 580
  29.3 2.2 copy-start.33
  30.1 1.5 copy-start.35
  48.5 28.7 %copy-start.21 = (f32[512,8,96]{0,2,1:T(8,128)S(1)}, f32[512,8,96]{0,2,1:T(8,128)}, u32[]{:S(2)}) copy-start(f32[512,8,96]{0,2,1:T(8,128)} %fusion.45) | copy-start | bytes 4718596
  113.2 6.8 copy-start.22
  124.7 1.4 copy-start.13
  129.3 76.1 %all-to-all-start = ((bf16[2,256,3072]{1,0,2:T(2,128)(2,1)}), bf16[2,256,3072]{1,0,2:T(2,128)(2,1)S(1)}, u32[]{:S(2)}, u32[]{:S(2)}) async-start(bf16[2,256,3072]{1,0,2:T(2,128)(2,1)} %reshape.346), calls=%async_computation | async-start | bytes 6291456 | tf_op jit(solution)/shard_map/all_to_all | solution.py:192
  215.4 3.8 copy-start.2
  230.0 3.8 copy-start.2
  249.3 41.2 %all-to-all-start.1 = ((bf16[2,1024,384]{2,0,1:T(2,128)(2,1)}), bf16[2,1024,384]{2,0,1:T(2,128)(2,1)}, u32[]{:S(2)}, u32[]{:S(2)}) async-start(bf16[2,1024,384]{2,0,1:T(2,128)(2,1)} %copy.76), calls=%async_computation.1 | async-start | bytes 3145728 | tf_op jit(solution)/shard_map/all_to_all | solution.py:194
  301.0 1.7 copy-start.8
  394.5 11.0 copy-start.9
  405.4 12.0 copy-start.6
  418.2 7.3 copy-start.7
  430.4 42.1 %all-to-all-start.2 = ((bf16[2,256,1536]{1,0,2:T(2,128)(2,1)}), bf16[2,256,1536]{1,0,2:T(2,128)(2,1)}, u32[]{:S(2)}, u32[]{:S(2)}) async-start(bf16[2,256,1536]{1,0,2:T(2,128)(2,1)} %copy.78), calls=%async_computation.2 | async-start | bytes 3145728 | tf_op jit(solution)/shard_map/all_to_all | solution.py:262
  435.0 275.9 %reduce-scatter.8.cloned.1.call-start = ((), (), s32[]{:S(2)}) async-start(), calls=%async_computation.18 | async-start | bytes 5308416 | tf_op jit(solution)/shard_map/reduce_scatter | solution.py:293
  472.5 7.7 copy-start.38
  490.9 10.0 copy-start.4
  504.2 2.9 copy-start.5
  507.2 8.3 copy-start.3
  527.2 10.0 copy-start.4
  540.5 2.9 copy-start.5
  543.4 8.3 copy-start.3
  650.3 2.0 copy-start.23
  650.4 1.1 copy-start.19
  656.7 109.3 %reduce-scatter.14.cloned.1.call-start = ((), (), s32[]{:S(2)}) async-start(), calls=%async_computation.21 | async-start | bytes 5308416 | tf_op jit(solution)/shard_map/reduce_scatter | solution.py:302
  664.1 148.2 %reduce-scatter.10.cloned.1.call-start = ((), (), s32[]{:S(2)}) async-start(), calls=%async_computation.19 | async-start | bytes 2654208 | tf_op jit(solution)/shard_map/reduce_scatter | solution.py:296
  664.1 1.9 copy-start.24
  666.0 2.9 copy-start.14
  666.0 2.9 copy-start.25
  668.9 189.6 %reduce-scatter.12.cloned.1.call-start = ((), (), s32[]{:S(2)}) async-start(), calls=%async_computation.20 | async-start | bytes 2654208 | tf_op jit(solution)/shard_map/reduce_scatter | solution.py:299
  671.8 282.4 %reduce-scatter.16.cloned.1.call-start = ((), (), s32[]{:S(2)}) async-start(), calls=%async_computation.22 | async-start | bytes 14155776 | tf_op jit(solution)/shard_map/reduce_scatter | solution.py:244
  683.6 1.5 copy-start.27
  683.7 366.4 %reduce-scatter.18.cloned.1.call-start = ((), (), s32[]{:S(2)}) async-start(), calls=%async_computation.23 | async-start | bytes 14155776 | tf_op jit(solution)/shard_map/reduce_scatter | solution.py:247
  697.1 1.4 copy-start.26
  697.1 448.6 %reduce-scatter.20.cloned.1.call-start = ((), (), s32[]{:S(2)}) async-start(), calls=%async_computation.24 | async-start | bytes 14155776 | tf_op jit(solution)/shard_map/reduce_scatter | solution.py:250
  710.9 491.4 %all-gather.24.cloned.1.call-start = ((), (), s32[]{:S(2)}) async-start(), calls=%async_computation.25 | async-start | bytes 2949120 | tf_op jit(solution)/shard_map/all_gather | solution.py:309
  710.9 435.3 %copy-start.10 = (f32[512,1536]{1,0:T(8,128)S(1)}, f32[512,1536]{1,0:T(8,128)}, u32[]{:S(2)}) copy-start(f32[512,1536]{1,0:T(8,128)} %copy-done.8) | copy-start | bytes 9437188
  711.5 697.6 %all-reduce.10.cloned.1.call-start = ((), (), s32[]{:S(2)}) async-start(), calls=%async_computation.26 | async-start | bytes 11796480 | tf_op jit(solution)/shard_map/psum | solution.py:312
  1146.3 12.4 copy-start.20
  1158.7 4.7 copy-start.11
  1158.7 4.7 copy-start.17
  1163.4 1.9 copy-start.1
  1163.4 2.1 copy-start.15
  1163.5 2.9 copy-start.18
  1163.5 2.9 copy-start.34
  1163.5 2.9 copy-start.36
  1166.3 3.7 copy-start.39
  1409.1 3.6 copy-start.29
  1412.6 2.0 copy-start.28
  1414.7 2.1 copy-start.30
  1414.7 3.2 copy-start.32
  1414.7 4.1 copy-start.31
  (2 other events, 2.0 us)
Sparse Core Ops, SparseCore 0:
  9.9 31.8 all-gather.11
  43.6 28.8 all-gather.13
  74.4 38.7 all-gather.9
  115.0 38.7 all-gather.15
  155.5 71.9 all-gather.17
  229.3 71.9 all-gather.19
  303.2 71.9 all-gather.21
  656.8 51.9 reduce-scatter.7
  712.3 53.7 reduce-scatter.13
  769.8 42.3 reduce-scatter.9
  816.1 42.3 reduce-scatter.11
  861.9 92.3 reduce-scatter.15
  957.7 92.2 reduce-scatter.17
  1053.4 92.2 reduce-scatter.19
  1147.1 50.2 all-gather.23
  1200.1 208.9 all-reduce.9
